TPU v7x, 256 devices: a whole 4x4x8 slice. The times are simulated.
256 devices in a mesh: grp: 2 (over core), dp: 128 (over z, y, x).
Axes of the slice: x: 4, y: 4, z: 8, core: 2. Of those that a mesh axis runs over, the one named last changes fastest.
Arguments:
- version_tags: int32 [262144], P(('grp', 'dp')), may hold values from 0 to 3
- packed_pos: int32 [262144], P(('grp', 'dp')), may hold values from 0 to 262143, as said below
- valid_mask: int32 [262144, 128], P(('grp', 'dp')), may hold values from 0 to 1, as said below
- returns: float32 [262144, 128], P(('grp', 'dp')), may hold values from -16 to 16
- values: float32 [262144, 128], P(('grp', 'dp')), may hold values from -6 to 6
- log_ratio_new: float32 [262144, 128], P(('grp', 'dp')), may hold values from -4 to 4
- log_ratio_prox: float32 [262144, 128], P(('grp', 'dp')), may hold values from -4 to 4
Outputs:
- token_loss: float32 [262144, 128], P(('grp', 'dp'))
- block_loss: float32 [262144], P(('grp', 'dp'))
Inputs may be any that keep to these rules, and one draw needn't show every extreme that they name: `packed_pos`: A permutation of the blocks. Blocks stay within their group of 128 devices along dp; each device's 1024 packed positions take 1024 // 128 blocks from every device of its group, those of the s-th device of the group at local packed positions s * (8) onward; which of a device's blocks go where is otherwise arbitrary. `valid_mask`: some blocks have no valid token.
All inputs are finite; a program needn't handle non-finite values.
Results may differ from a plain program's by a relative error of at most 0.00002.
Values sent between devices are 32-bit elements; how exact they have to be, the bound alone decides.
A program may use at most 64 MiB of HBM per device.

v0:
```python
import functools

import jax
import jax.numpy as jnp
from jax import lax
from jax.sharding import Mesh
from jax.sharding import PartitionSpec as P

VERSIONS = 4
DP = ("dp_0", "dp_1", "dp_2")
GRP_DP = ("grp", "dp_0", "dp_1", "dp_2")


def by_axis(array, axes):
    return functools.reduce(lax.psum, axes, array)


def one_hot_of(labels):
    return (labels[:, None] == jnp.arange(VERSIONS)[None, :]).astype(jnp.float32)


def surrogate(prob_ratio, weight, white):
    clipped = jnp.clip(prob_ratio, 0.8, 1.2)
    return -weight * jnp.minimum(prob_ratio * white, clipped * white)


def on_device(version_tags, packed_pos, valid_mask, returns, values, log_ratio_new, log_ratio_prox):
    blk_dev = version_tags.shape[0]
    n_peers = lax.axis_size(DP)
    per_peer = blk_dev // n_peers
    advantage = returns - values
    maskf = valid_mask.astype(jnp.float32)
    onehot = one_hot_of(version_tags)
    block_count = jnp.sum(maskf, axis=1)
    counts = jnp.sum(onehot * block_count[:, None], axis=0)
    adv_sums = jnp.sum(onehot * jnp.sum(maskf * advantage, axis=1)[:, None], axis=0)
    prob_ratio = jnp.exp(log_ratio_new)
    weight = maskf * jnp.exp(log_ratio_prox)
    local_packed = packed_pos % blk_dev
    target = packed_pos // blk_dev % n_peers
    send_index = target * per_peer + local_packed - lax.axis_index(DP) * per_peer

    def place(array):
        return jnp.zeros_like(array).at[send_index].set(array)

    raw_sq = jnp.sum(onehot * jnp.sum(maskf * advantage * advantage, axis=1)[:, None], axis=0)
    total_count, total_sum, total_sq = (
        by_axis(counts, GRP_DP),
        by_axis(adv_sums, GRP_DP),
        by_axis(raw_sq, GRP_DP),
    )
    version_mean = total_sum / jnp.maximum(total_count, 1.0)
    squares = total_sq - total_sum * version_mean
    version_scale = 1.0 / jnp.sqrt(squares / jnp.maximum(total_count, 1.0) + 0.05)
    block_mean = jnp.sum(onehot * version_mean[None, :], axis=1)
    block_scale = jnp.sum(onehot * version_scale[None, :], axis=1)
    white = (advantage - block_mean[:, None]) * block_scale[:, None]
    local_loss = surrogate(prob_ratio, weight, white)
    local_block = jnp.sum(local_loss, axis=1) / jnp.maximum(block_count, 1.0)
    token_loss, block_loss = (
        lax.all_to_all(place(local_loss), DP, split_axis=0, concat_axis=0, tiled=True),
        lax.all_to_all(place(local_block), DP, split_axis=0, concat_axis=0, tiled=True),
    )
    return (token_loss, block_loss)


def solution(mesh):
    split = Mesh(mesh.devices.reshape(mesh.shape["grp"], 8, 4, 4), ("grp", "dp_0", "dp_1", "dp_2"))
    placed = (
        P(GRP_DP),
        P(GRP_DP),
        P(GRP_DP, None),
        P(GRP_DP, None),
        P(GRP_DP, None),
        P(GRP_DP, None),
        P(GRP_DP, None),
    )
    return jax.shard_map(
        on_device,
        mesh=split,
        in_specs=placed,
        out_specs=(P(GRP_DP, None), P(GRP_DP)),
        check_vma=False,
    )
```

profile of v0, /device:TPU:32, one launch (start us, length us, event | category | flops | bytes accessed | tf_op | source)
XLA Modules:
  0.0 94.2 jit_solution(370029366914854639)
XLA Ops:
  0.6 0.0 copy-start
  0.6 0.0 copy-start.1
  0.7 0.0 copy-start.2
  0.7 2.0 %fusion = (f32[1024]{0:T(1024)S(1)}, f32[1024]{0:T(1024)S(1)}, f32[1024]{0:T(1024)S(1)}, f32[1024,128]{1,0:T(8,128)S(1)}) fusion(s32[1024,128]{1,0:T(8,128)} %param.9, f32[1024,128]{1,0:T(8,128)} %param.10, f32[1024,128]{1,0:T(8,128)} %param.11), kind=kLoop, calls=%fused_computation.6 | loop fusion | flops 914432 | bytes 2109440 | tf_op jit(solution)/shard_map/reduce_sum | solution.py:36
  2.6 0.0 copy-start.3
  2.6 0.7 copy-done.3
  3.3 0.2 select_reduce_fusion.3
  3.5 2.5 %all-reduce.3 = (f32[4]{0:T(128)S(1)}, f32[4]{0:T(128)S(1)}, f32[4]{0:T(128)S(1)}) all-reduce(f32[4]{0:T(128)S(1)} %get-tuple-element.9, f32[4]{0:T(128)S(1)} %get-tuple-element.7, f32[4]{0:T(128)S(1)} %get-tuple-element.8), channel_id=1, replica_groups=mesh['grp'=2,'dp_0'=8,'dp_1'=4,'dp_2'=4] {'grp'}, use_global_device_ids=true, to_apply=%region_2.0 | all-reduce | flops 12 | bytes 96 | tf_op jit(solution)/shard_map/psum | solution.py:15
  5.9 17.9 %all-reduce = (f32[4]{0:T(128)S(1)}, f32[4]{0:T(128)S(1)}, f32[4]{0:T(128)S(1)}) all-reduce(f32[4]{0:T(128)S(1)} %get-tuple-element.19, f32[4]{0:T(128)S(1)} %get-tuple-element.20, f32[4]{0:T(128)S(1)} %get-tuple-element.21), channel_id=1, replica_groups=mesh['grp'=2,'dp_0'=8,'dp_1'=4,'dp_2'=4] {'dp_0'}, use_global_device_ids=true, to_apply=%region_3.0 | all-reduce | flops 12 | bytes 96 | tf_op jit(solution)/shard_map/psum | solution.py:15
  23.8 10.7 %all-reduce.2 = (f32[4]{0:T(128)S(1)}, f32[4]{0:T(128)S(1)}, f32[4]{0:T(128)S(1)}) all-reduce(f32[4]{0:T(128)S(1)} %get-tuple-element.10, f32[4]{0:T(128)S(1)} %get-tuple-element.11, f32[4]{0:T(128)S(1)} %get-tuple-element.12), channel_id=1, replica_groups=mesh['grp'=2,'dp_0'=8,'dp_1'=4,'dp_2'=4] {'dp_1'}, use_global_device_ids=true, to_apply=%region_4.5 | all-reduce | flops 12 | bytes 96 | tf_op jit(solution)/shard_map/psum | solution.py:15
  34.5 10.5 %all-reduce.1 = (f32[4]{0:T(128)S(1)}, f32[4]{0:T(128)S(1)}, f32[4]{0:T(128)S(1)}) all-reduce(f32[4]{0:T(128)S(1)} %get-tuple-element.16, f32[4]{0:T(128)S(1)} %get-tuple-element.17, f32[4]{0:T(128)S(1)} %get-tuple-element.18), channel_id=1, replica_groups=mesh['grp'=2,'dp_0'=8,'dp_1'=4,'dp_2'=4] {'dp_2'}, use_global_device_ids=true, to_apply=%region_5.6 | all-reduce | flops 12 | bytes 96 | tf_op jit(solution)/shard_map/psum | solution.py:15
  45.0 0.1 select_reduce_fusion.2
  45.1 0.0 copy-done
  45.2 0.0 copy-done.1
  45.2 0.0 copy-done.2
  45.2 0.5 fusion.10
  45.7 0.0 copy-start.4
  45.7 0.7 copy-done.4
  46.4 4.3 %scatter_custom_fusion.1 = f32[1024]{0:T(1024)S(1)} fusion(s32[1024]{0:T(1024)S(1)} %compare_select_fusion, f32[1024]{0:T(1024)S(1)} %maximum_divide_fusion, f32[]{:T(128)} %constant.59.clone.1), kind=kCustom, calls=%fused_computation.31 | custom fusion | bytes 4100 | tf_op jit(solution)/shard_map/scatter | solution.py:44
  50.7 0.7 all_to_all.19
  51.4 7.8 %all-to-all-start.1 = ((f32[128,8,1]{1,2,0:T(1,128)}), f32[128,8,1]{1,2,0:T(1,128)S(1)}, u32[]{:S(2)}, u32[]{:S(2)}) async-start(f32[128,8,1]{1,2,0:T(1,128)} %bitcast.2), calls=%async_computation.1 | async-start | bytes 131072 | tf_op jit(solution)/shard_map/all_to_all | solution.py:62
  59.2 3.9 %scatter_custom_fusion = f32[1024,128]{1,0:T(8,128)} fusion(s32[1024]{0:T(1024)S(1)} %compare_select_fusion, f32[1024,128]{1,0:T(8,128)S(1)} %get-tuple-element.23, f32[]{:T(128)} %constant.59.clone.1), kind=kCustom, calls=%fused_computation.7 | custom fusion | bytes 524292 | tf_op jit(solution)/shard_map/scatter | solution.py:44
  63.1 7.6 %all-to-all-done.1 = f32[128,8,1]{1,2,0:T(1,128)S(1)} async-done(((f32[128,8,1]{1,2,0:T(1,128)}), f32[128,8,1]{1,2,0:T(1,128)S(1)}, u32[]{:S(2)}, u32[]{:S(2)}) %all-to-all-start.1) | async-done | bytes 4128 | tf_op jit(solution)/shard_map/all_to_all | solution.py:62
  70.7 6.6 %all-to-all-start = ((f32[128,8,128]{2,1,0:T(8,128)}), f32[128,8,128]{2,1,0:T(8,128)S(1)}, u32[]{:S(2)}, u32[]{:S(2)}) async-start(f32[128,8,128]{2,1,0:T(8,128)} %bitcast), calls=%async_computation | async-start | bytes 1048576 | tf_op jit(solution)/shard_map/all_to_all | solution.py:61
  77.3 0.5 broadcast.53
  77.8 0.8 reduce.3
  78.6 0.7 all_to_all.21
  79.3 14.1 %all-to-all-done = f32[128,8,128]{2,1,0:T(8,128)S(1)} async-done(((f32[128,8,128]{2,1,0:T(8,128)}), f32[128,8,128]{2,1,0:T(8,128)S(1)}, u32[]{:S(2)}, u32[]{:S(2)}) %all-to-all-start) | async-done | bytes 524320 | tf_op jit(solution)/shard_map/all_to_all | solution.py:61
  93.4 0.8 copy.12
  (3 shorter events, 0.0 us)
Async XLA Ops:
  0.6 44.5 %copy-start = (s32[1024,128]{1,0:T(8,128)S(1)}, s32[1024,128]{1,0:T(8,128)}, u32[]{:S(2)}) copy-start(s32[1024,128]{1,0:T(8,128)} %param.9) | copy-start | bytes 1572868
  0.6 44.5 %copy-start.1 = (f32[1024,128]{1,0:T(8,128)S(1)}, f32[1024,128]{1,0:T(8,128)}, u32[]{:S(2)}) copy-start(f32[1024,128]{1,0:T(8,128)} %param.12) | copy-start | bytes 1572868
  0.7 44.5 %copy-start.2 = (f32[1024,128]{1,0:T(8,128)S(1)}, f32[1024,128]{1,0:T(8,128)}, u32[]{:S(2)}) copy-start(f32[1024,128]{1,0:T(8,128)} %param.13) | copy-start | bytes 1572868
  2.6 0.7 copy-start.3
  45.7 0.7 copy-start.4
  51.4 19.3 %all-to-all-start.1 = ((f32[128,8,1]{1,2,0:T(1,128)}), f32[128,8,1]{1,2,0:T(1,128)S(1)}, u32[]{:S(2)}, u32[]{:S(2)}) async-start(f32[128,8,1]{1,2,0:T(1,128)} %bitcast.2), calls=%async_computation.1 | async-start | bytes 131072 | tf_op jit(solution)/shard_map/all_to_all | solution.py:62
  70.7 22.8 %all-to-all-start = ((f32[128,8,128]{2,1,0:T(8,128)}), f32[128,8,128]{2,1,0:T(8,128)S(1)}, u32[]{:S(2)}, u32[]{:S(2)}) async-start(f32[128,8,128]{2,1,0:T(8,128)} %bitcast), calls=%async_computation | async-start | bytes 1048576 | tf_op jit(solution)/shard_map/all_to_all | solution.py:61
where the time goes:
time: 94.8 us; the launch traced here: 94.2 us
  blocking collectives  41.5 us (44%)
  waiting for transfers between devices  21.7 us (23%)
  starting transfers between devices  14.4 us (15%)
  local copies, waits for them, and re-layouts  12.2 us (13%)
  other arithmetic  3.56 us (4%)
    psum x4, blocking collectives, by_axis(): return functools.reduce(lax.psum, axes, array)  41.5 us
    all_to_all x1, waiting for transfers between devices, on_device(): lax.all_to_all(place(local_loss), DP, split_axis=0, concat_axis=0, tiled=...  14.1 us
    scatter x2, local copies, waits for them, and re-layouts, place(): return jnp.zeros_like(array).at[send_index].set(array)  8.17 us
    all_to_all x1, starting transfers between devices, on_device(): lax.all_to_all(place(local_block), DP, split_axis=0, concat_axis=0, tiled...  7.79 us
    all_to_all x1, waiting for transfers between devices, on_device(): lax.all_to_all(place(local_block), DP, split_axis=0, concat_axis=0, tiled...  7.59 us
    all_to_all x1, starting transfers between devices, on_device(): lax.all_to_all(place(local_loss), DP, split_axis=0, concat_axis=0, tiled=...  6.61 us
    unnamed x11, local copies, waits for them, and re-layouts  2.16 us
    reduce_sum x1, other arithmetic, on_device(): jnp.sum(maskf * advantage, axis=1)[:, None]  1.97 us
  transfers between devices with their start and end apart: 2, of which 2 were waited for; matrix products, arithmetic and copies ran while one was open for 5% of the time, Pallas kernels for 0%

commit v1 on v0

v1 whole, which is shorter than its diff:
```python
import functools

import jax
import jax.numpy as jnp
from jax import lax
from jax.experimental import pallas as pl
from jax.experimental.pallas import tpu as pltpu
from jax.sharding import Mesh
from jax.sharding import PartitionSpec as P

MESH = pl.DeviceIdType.MESH
VERSIONS = 4
LANES = 128
AXES = ("grp", "z", "y", "x")
FAR4 = (2, 1, 3, 0)
FAR8 = (4, 3, 5, 2, 6, 1, 7, 0)


def split3(value):
    high = value.astype(jnp.bfloat16)
    rest = value - high.astype(jnp.float32)
    middle = rest.astype(jnp.bfloat16)
    low = (rest - middle.astype(jnp.float32)).astype(jnp.bfloat16)
    return high, middle, low


def combine(moments):
    count = sum(m[0] for m in moments)
    total = sum(m[0] * m[1] for m in moments)
    mean = total / jnp.maximum(count, 1.0)
    square = sum(m[2] + m[0] * (m[1] - mean) * (m[1] - mean) for m in moments)
    return count, mean, square


def total_of(array):
    return jnp.sum(jnp.sum(array, axis=0, keepdims=True), axis=1, keepdims=True)


def kernel(
    tags_h, packed_h, mask_h, returns_h, values_h, new_h, prox_h,
    token_o, block_o,
    tags, packed, mask, returns, values, new, prox,
    per_block, onehot, side, pieces, placed, loss,
    msg_a, msg_b, got_a, got_b,
    packed_count, got_count, count_rows, got_rows,
    load_sem, stat_send, stat_recv, count_send, count_recv, token_send, token_recv,
):
    g, z, y, x = (lax.axis_index(name) for name in AXES)
    n_z, n_y, n_x = (lax.axis_size(name) for name in AXES[1:])
    plane = n_y * n_x
    blocks = mask.shape[0]
    chunk = blocks // n_z
    per_peer = blocks // (n_z * plane)
    here = y * n_x + x
    me = z * plane + here

    loads = [
        pltpu.make_async_copy(src, dst, load_sem.at[i])
        for i, (src, dst) in enumerate(
            [(returns_h, returns), (values_h, values), (mask_h, mask), (tags_h, tags), (packed_h, packed), (new_h, new), (prox_h, prox)]
        )
    ]
    for load in loads:
        load.start()

    def at(dg, dz, dy, dx):
        return (g ^ dg, lax.rem(z + dz, n_z), lax.rem(y + dy, n_y), lax.rem(x + dx, n_x))

    near = [(dg, 0, dy, dx) for dg in (0, 1) for dy in FAR4 for dx in FAR4][:]
    near = [o for o in near if o != (0, 0, 0, 0)]
    line = [(0, dz, 0, 0) for dz in FAR8 if dz]

    barrier = pltpu.get_barrier_semaphore()
    for o in near + line:
        pl.semaphore_signal(barrier, inc=1, device_id=at(*o), device_id_type=MESH)

    for load in loads[:4]:
        load.wait()
    for s in range(n_z):
        rows = pl.ds(s * chunk, chunk)
        valid = mask[rows, :].astype(jnp.float32).T
        advantage = (returns[rows, :] - values[rows, :]).T
        count = jnp.sum(valid, axis=0, keepdims=True)
        mean = jnp.sum(valid * advantage, axis=0, keepdims=True) / jnp.maximum(count, 1.0)
        centred = advantage - mean
        per_block[0, s : s + 1, :] = count
        per_block[1, s : s + 1, :] = mean
        per_block[2, s : s + 1, :] = jnp.sum(valid * centred * centred, axis=0, keepdims=True)

    lane = lax.broadcasted_iota(jnp.int32, (1, LANES), 1)
    tag = tags[...]
    count, mean, square = per_block[0], per_block[1], per_block[2]
    local = [jnp.zeros((1, LANES), jnp.float32)] * 3
    for v in range(VERSIONS):
        mine = tag == v
        count_v = total_of(jnp.where(mine, count, 0.0))
        mean_v = total_of(jnp.where(mine, count * mean, 0.0)) / jnp.maximum(count_v, 1.0)
        square_v = total_of(jnp.where(mine, square + count * (mean - mean_v) * (mean - mean_v), 0.0))
        local = [jnp.where(lane == v, new_value, old) for new_value, old in zip((count_v, mean_v, square_v), local)]
    own_a = g * plane + here
    for k in range(3):
        msg_a[k] = local[k]
        got_a[own_a, k] = local[k]

    pl.semaphore_wait(barrier, len(near) + len(line))
    for o in near:
        pltpu.make_async_remote_copy(
            src_ref=msg_a, dst_ref=got_a.at[own_a], send_sem=stat_send.at[0], recv_sem=stat_recv.at[0],
            device_id=at(*o), device_id_type=MESH,
        ).start()

    def bytes_of(ref, send, recv):
        return pltpu.make_async_remote_copy(src_ref=ref, dst_ref=ref, send_sem=send, recv_sem=recv, device_id=(g, z, y, x), device_id_type=MESH)

    all_a = bytes_of(got_a.at[pl.ds(0, len(near))], stat_send.at[0], stat_recv.at[0])
    all_a.wait_recv()
    merged = combine([[got_a[i, k] for k in range(3)] for i in range(2 * plane)])
    for k in range(3):
        msg_b[k] = merged[k]
        got_b[z, k] = merged[k]
    for o in line:
        pltpu.make_async_remote_copy(
            src_ref=msg_b, dst_ref=got_b.at[z], send_sem=stat_send.at[1], recv_sem=stat_recv.at[1],
            device_id=at(*o), device_id_type=MESH,
        ).start()

    loads[4].wait()
    where = packed[...]
    target = lax.rem(where // blocks, n_z * plane)
    order = target * per_peer + lax.rem(where, blocks) - me * per_peer
    for s in range(n_z):
        rows = pl.ds(s * chunk, chunk)
        tag_rows = jnp.broadcast_to(tag[s : s + 1, :].astype(jnp.float32), (chunk, LANES)).T
        count_cols = jnp.broadcast_to(count[s : s + 1, :], (chunk, LANES)).T
        side[rows, 0:LANES] = tag_rows.astype(jnp.bfloat16)
        side[rows, LANES : 2 * LANES] = count_cols.astype(jnp.bfloat16)

    tag_at, min_at, max_at, adv_at = 0, 1, 2, 3

    @pl.loop(0, n_z)
    def _(c):
        rows = pl.ds(pl.multiple_of(c * chunk, chunk), chunk)
        slot = lax.broadcasted_iota(jnp.int32, (chunk, LANES), 0) + c * chunk
        for s in range(n_z):
            hit = jnp.broadcast_to(order[s : s + 1, :], (chunk, LANES)) == slot
            onehot[rows, s * LANES : (s + 1) * LANES] = jnp.where(hit, 1.0, 0.0).astype(jnp.bfloat16)
        moved = jnp.dot(onehot[rows, :], side[...], preferred_element_type=jnp.float32)
        placed[tag_at, rows, :] = moved[:, 0:LANES]
        packed_count[pl.ds(c, 1), :] = moved[:, LANES : 2 * LANES].T[0:1, :]

    for o in near:
        if o[0] == 0:
            pltpu.make_async_remote_copy(
                src_ref=packed_count, dst_ref=got_count.at[here], send_sem=count_send.at[0], recv_sem=count_recv.at[0],
                device_id=at(*o), device_id_type=MESH,
            ).start()
    got_count[here] = packed_count[...]

    for load in loads[5:]:
        load.wait()

    @pl.loop(0, n_z)
    def _(s):
        rows = pl.ds(pl.multiple_of(s * chunk, chunk), chunk)
        ratio = jnp.exp(new[rows, :])
        weight = mask[rows, :].astype(jnp.float32) * jnp.exp(prox[rows, :])
        parts = split3(weight * jnp.minimum(ratio, 1.2))
        parts += split3(weight * jnp.maximum(ratio, 0.8))
        parts += split3(returns[rows, :] - values[rows, :])
        for k, part in enumerate(parts):
            pieces[rows, k * LANES : (k + 1) * LANES] = part

    @pl.loop(0, n_z)
    def _(c):
        rows = pl.ds(pl.multiple_of(c * chunk, chunk), chunk)
        moved = jnp.dot(onehot[rows, :], pieces[...], preferred_element_type=jnp.float32)
        for k in range(3):
            high, middle, low = (moved[:, (3 * k + i) * LANES : (3 * k + i + 1) * LANES] for i in range(3))
            placed[min_at + k, rows, :] = high + middle + low

    bytes_of(got_count.at[pl.ds(0, plane - 1)], count_send.at[0], count_recv.at[0]).wait_recv()
    lanes8 = lax.broadcasted_iota(jnp.int32, (n_z, LANES), 1) // per_peer
    gathered = jnp.zeros((n_z, LANES), jnp.float32)
    for p in range(plane):
        turn = lax.rem((p - here + plane) * per_peer, LANES)
        gathered = jnp.where(lanes8 == p, pltpu.roll(got_count[p], turn, 1), gathered)
    for r in range(n_z):
        count_rows[r] = gathered[r : r + 1, :]
    got_rows[z] = count_rows[z]
    for o in line:
        device = at(*o)
        pltpu.make_async_remote_copy(
            src_ref=count_rows.at[device[1]], dst_ref=got_rows.at[z], send_sem=count_send.at[1], recv_sem=count_recv.at[1],
            device_id=device, device_id_type=MESH,
        ).start()

    all_b = bytes_of(got_b.at[pl.ds(0, len(line))], stat_send.at[1], stat_recv.at[1])
    all_b.wait_recv()
    count, mean, square = combine([[got_b[i, k] for k in range(3)] for i in range(n_z)])
    scale = 1.0 / jnp.sqrt(square / jnp.maximum(count, 1.0) + 0.05)

    def spread(row, v):
        return jnp.broadcast_to(jnp.sum(jnp.where(lane == v, row, 0.0), axis=1, keepdims=True), (chunk, LANES))

    means = [spread(mean, v) for v in range(VERSIONS)]
    scales = [spread(scale, v) for v in range(VERSIONS)]

    @pl.loop(0, n_z)
    def _(c):
        rows = pl.ds(pl.multiple_of(c * chunk, chunk), chunk)
        tag_c = placed[tag_at, rows, :]
        mean_c, scale_c = means[0], scales[0]
        for v in range(1, VERSIONS):
            mean_c = jnp.where(tag_c == v, means[v], mean_c)
            scale_c = jnp.where(tag_c == v, scales[v], scale_c)
        white = (placed[adv_at, rows, :] - mean_c) * scale_c
        factor = jnp.where(white >= 0.0, placed[min_at, rows, :], placed[max_at, rows, :])
        loss[rows, :] = -(factor * white)

    own = pl.ds(pl.multiple_of(me * per_peer, per_peer), per_peer)
    for dy in FAR4:
        for dx in FAR4:
            for dz in FAR8:
                if (dz, dy, dx) != (0, 0, 0):
                    device = at(0, dz, dy, dx)
                    there = (device[1] * plane + device[2] * n_x + device[3]) * per_peer
                    pltpu.make_async_remote_copy(
                        src_ref=loss.at[pl.ds(pl.multiple_of(there, per_peer), per_peer)], dst_ref=token_o.at[own],
                        send_sem=token_send, recv_sem=token_recv.at[z], device_id=device, device_id_type=MESH,
                    ).start()
    token_o[own, :] = loss[own, :]

    bytes_of(got_rows.at[pl.ds(0, len(line))], count_send.at[1], count_recv.at[1]).wait_recv()
    for dz in (0, 1, 7, 2, 6, 3, 5, 4):
        src = lax.rem(z + dz, n_z)
        expect = blocks // n_z - (per_peer if dz == 0 else 0)
        bytes_of(token_o.at[pl.ds(0, expect)], token_send, token_recv.at[src]).wait_recv()
        rows = pl.ds(pl.multiple_of(src * chunk, chunk), chunk)
        sums = jnp.sum(token_o[rows, :].T, axis=0, keepdims=True)
        block_o[pl.ds(src, 1), :] = sums / jnp.maximum(got_rows[src], 1.0)

    bytes_of(got_a.at[pl.ds(0, len(near))], stat_send.at[0], stat_recv.at[0]).wait_send()
    bytes_of(got_b.at[pl.ds(0, len(line))], stat_send.at[1], stat_recv.at[1]).wait_send()
    bytes_of(got_count.at[pl.ds(0, plane - 1)], count_send.at[0], count_recv.at[0]).wait_send()
    bytes_of(got_rows.at[pl.ds(0, len(line))], count_send.at[1], count_recv.at[1]).wait_send()
    bytes_of(token_o.at[pl.ds(0, blocks - per_peer)], token_send, token_recv.at[0]).wait_send()


def on_device(version_tags, packed_pos, valid_mask, returns, values, log_ratio_new, log_ratio_prox):
    blocks, tokens = valid_mask.shape
    n_z, n_y, n_x = (lax.axis_size(name) for name in AXES[1:])
    plane = n_y * n_x
    f32, i32, bf16 = jnp.float32, jnp.int32, jnp.bfloat16
    vmem, dma = pltpu.VMEM, pltpu.SemaphoreType.DMA
    small = (blocks // LANES, LANES)
    token_loss, block_loss = pl.pallas_call(
        kernel,
        out_shape=(pltpu.VMEM((blocks, tokens), f32), pltpu.VMEM(small, f32)),
        in_specs=[pl.BlockSpec(memory_space=pltpu.HBM)] * 7,
        out_specs=[pl.BlockSpec(memory_space=pltpu.VMEM)] * 2,
        scratch_shapes=[
            vmem(small, i32), vmem(small, i32), vmem((blocks, tokens), i32),
            *[vmem((blocks, tokens), f32)] * 4,
            vmem((3, *small), f32), vmem((blocks, blocks), bf16), vmem((blocks, 2 * LANES), bf16), vmem((blocks, 9 * LANES), bf16),
            vmem((4, blocks, LANES), f32), vmem((blocks, LANES), f32),
            vmem((3, 1, LANES), f32), vmem((3, 1, LANES), f32), vmem((2 * plane, 3, 1, LANES), f32), vmem((n_z, 3, 1, LANES), f32),
            vmem(small, f32), vmem((plane, *small), f32), vmem((n_z, 1, LANES), f32), vmem((n_z, 1, LANES), f32),
            dma((7,)), dma((2,)), dma((2,)), dma((2,)), dma((2,)), dma, dma((n_z,)),
        ],
        compiler_params=pltpu.CompilerParams(collective_id=0, has_side_effects=True, vmem_limit_bytes=32 * 2**20),
    )(*[pltpu.with_memory_space_constraint(a, pltpu.HBM) for a in (version_tags.reshape(small), packed_pos.reshape(small), valid_mask, returns, values, log_ratio_new, log_ratio_prox)])
    return token_loss, block_loss.reshape(blocks)


def solution(mesh):
    split = Mesh(mesh.devices.reshape(mesh.shape["grp"], 8, 4, 4), AXES)
    row, flat = P(AXES, None), P(AXES)
    return jax.shard_map(
        on_device,
        mesh=split,
        in_specs=(flat, flat, row, row, row, row, row),
        out_specs=(row, flat),
        check_vma=False,
    )
```

time: 94.8 us -> 40.1 us (0.42)
  the two profiles are of different devices: /device:TPU:32 before, /device:TPU:1 now
where the time goes in v1:
time: 40.1 us; the launch traced here: 40 us
  Pallas kernels  38 us (95%)
  local copies, waits for them, and re-layouts  1.39 us (3%)
  between operations  0.64 us (2%)
    pallas_call x1, Pallas kernels, on_device(): pl.pallas_call(kernel, out_shape=(pltpu.VMEM((blocks, tokens), f32), pltp...  38 us
    unnamed x2, local copies, waits for them, and re-layouts  1.39 us

profile of v1, /device:TPU:1, one launch (start us, length us, event | category | flops | bytes accessed | tf_op | source)
XLA Modules:
  0.0 40.0 jit_solution(15786703948363079258)
XLA Ops:
  0.6 38.0 %shard_map.86 = (f32[1024,128]{1,0:T(8,128)S(1)}, f32[8,128]{1,0:T(8,128)S(1)}) custom-call(s32[8,128]{1,0:T(8,128)} %bitcast.4, s32[8,128]{1,0:T(8,128)} %bitcast.5, s32[1024,128]{1,0:T(8,128)} %mask_h.1, f32[1024,128]{1,0:T(8,128)} %returns_h.1, f32[1024,128]{1,0:T(8,128)} %values_h.1, f32[1024,128]{1,0:T(8,128)} %new_h.1, f32[1024,128]{1,0:T(8,128)} %prox_h.1), custom_call_target="tpu_custom_call" | custom-call | tf_op jit(solution)/shard_map/pallas_call | solution.py:256
  38.6 0.8 %copy.11 = f32[1024,128]{1,0:T(8,128)} copy(f32[1024,128]{1,0:T(8,128)S(1)} %get-tuple-element.6) | data formatting | bytes 1048576
  39.4 0.6 %copy.12 = f32[1024]{0:T(1024)} copy(f32[1024]{0:T(1024)S(1)} %bitcast.3) | data formatting | bytes 8192

commit v2 on v1

v2 whole, which is shorter than its diff:
```python
import functools

import jax
import jax.numpy as jnp
from jax import lax
from jax.experimental import pallas as pl
from jax.experimental.pallas import tpu as pltpu
from jax.sharding import Mesh
from jax.sharding import PartitionSpec as P

MESH = pl.DeviceIdType.MESH
VERSIONS = 4
LANES = 128
AXES = ("grp", "z", "y", "x")
FAR4 = (2, 1, 3, 0)
FAR8 = (4, 3, 5, 2, 6, 1, 7, 0)


def combine(moments):
    count = sum(m[0] for m in moments)
    total = sum(m[0] * m[1] for m in moments)
    mean = total / jnp.maximum(count, 1.0)
    square = sum(m[2] + m[0] * (m[1] - mean) * (m[1] - mean) for m in moments)
    return count, mean, square


def total_of(array):
    return jnp.sum(jnp.sum(array, axis=0, keepdims=True), axis=1, keepdims=True)


def kernel(
    tags_h, packed_h, mask_h, returns_h, values_h, new_h, prox_h,
    token_o, block_o,
    tags, packed, mask, returns, values, new, prox,
    per_block, per_count, keys, kinds, placed, loss, inverse_v, inverse,
    msg_a, msg_b, got_a, got_b,
    packed_count, got_count, count_rows, got_rows,
    here_sem, part_sem, load_sem, scalar_sem, stat_send, stat_recv, count_send, count_recv, token_send, token_recv,
):
    g, z, y, x = (lax.axis_index(name) for name in AXES)
    n_z, n_y, n_x = (lax.axis_size(name) for name in AXES[1:])
    plane = n_y * n_x
    blocks = mask.shape[0]
    chunk = blocks // n_z
    per_peer = blocks // (n_z * plane)
    here = y * n_x + x
    me = z * plane + here

    parts = 4
    part = blocks // parts
    stat_loads = [
        [
            pltpu.make_async_copy(src.at[pl.ds(i * part, part)], dst.at[pl.ds(i * part, part)], part_sem.at[3 * i + k])
            for k, (src, dst) in enumerate([(mask_h, mask), (returns_h, returns), (values_h, values)])
        ]
        for i in range(parts)
    ]
    loads = [
        pltpu.make_async_copy(src, dst, load_sem.at[i])
        for i, (src, dst) in enumerate([(tags_h, tags), (packed_h, packed), (new_h, new), (prox_h, prox)])
    ]
    for load in sum(stat_loads, []) + loads[:2]:
        load.start()

    def at(dg, dz, dy, dx):
        return (g ^ dg, lax.rem(z + dz, n_z), lax.rem(y + dy, n_y), lax.rem(x + dx, n_x))

    flat = [(dg, 0, dy, dx) for dy in FAR4 for dx in FAR4 for dg in (1, 0) if (dg, dy, dx) != (0, 0, 0)]
    half = n_z // 2
    low = z < half

    def along(bits):
        return (g, z ^ bits, y, x)

    barrier = pltpu.get_barrier_semaphore()
    for o in flat:
        pl.semaphore_signal(barrier, inc=1, device_id=at(*o), device_id_type=MESH)
    for bits in range(1, half):
        pl.semaphore_signal(barrier, inc=1, device_id=along(bits), device_id_type=MESH)

    @pl.when(low)
    def _():
        for bits in range(half, n_z):
            pl.semaphore_signal(barrier, inc=1, device_id=along(bits), device_id_type=MESH)

    for s in range(n_z):
        rows = pl.ds(s * chunk, chunk)
        if s * chunk % part == 0:
            for load in stat_loads[s * chunk // part]:
                load.wait()
        valid = mask[rows, :].T
        per_count[s : s + 1, :] = jnp.sum(valid, axis=0, keepdims=True)
        valid = valid.astype(jnp.float32)
        advantage = (returns[rows, :] - values[rows, :]).T
        count = per_count[s : s + 1, :].astype(jnp.float32)
        mean = jnp.sum(valid * advantage, axis=0, keepdims=True) / jnp.maximum(count, 1.0)
        centred = advantage - mean
        per_block[0, s : s + 1, :] = count
        per_block[1, s : s + 1, :] = mean
        per_block[2, s : s + 1, :] = jnp.sum(valid * centred * centred, axis=0, keepdims=True)

    for load in loads[2:]:
        load.start()
    loads[0].wait()
    lane = lax.broadcasted_iota(jnp.int32, (1, LANES), 1)
    tag = tags[...]
    count, mean, square = per_block[0], per_block[1], per_block[2]
    local = [jnp.zeros((1, LANES), jnp.float32)] * 3
    for v in range(VERSIONS):
        mine = tag == v
        count_v = total_of(jnp.where(mine, count, 0.0))
        mean_v = total_of(jnp.where(mine, count * mean, 0.0)) / jnp.maximum(count_v, 1.0)
        square_v = total_of(jnp.where(mine, square + count * (mean - mean_v) * (mean - mean_v), 0.0))
        local = [jnp.where(lane == v, new_value, old) for new_value, old in zip((count_v, mean_v, square_v), local)]
    own_a = g * plane + here
    for k in range(3):
        msg_a[k] = local[k]
        got_a[own_a, k] = local[k]

    pl.semaphore_wait(barrier, len(flat) + half - 1 + jnp.where(low, 0, half))
    for o in flat:
        pltpu.make_async_remote_copy(
            src_ref=msg_a, dst_ref=got_a.at[own_a], send_sem=stat_send.at[0], recv_sem=stat_recv.at[0],
            device_id=at(*o), device_id_type=MESH,
        ).start()

    def bytes_of(ref, send, recv):
        return pltpu.make_async_remote_copy(src_ref=ref, dst_ref=ref, send_sem=send, recv_sem=recv, device_id=(g, z, y, x), device_id_type=MESH)

    @pl.when(jnp.logical_not(low))
    def _():
        for bits in range(half, n_z):
            pl.semaphore_signal(here_sem, inc=1, device_id=along(bits), device_id_type=MESH)

    loads[1].wait()
    where = packed[...]
    order = ((where // blocks) & (n_z * plane - 1)) * per_peer + (where & (blocks - 1)) - me * per_peer
    block = lax.broadcasted_iota(jnp.int32, order.shape, 0) * LANES + lax.broadcasted_iota(jnp.int32, order.shape, 1)
    value = block + blocks * (per_count[...] + 2 * LANES * tag)

    def columns(row):
        return jnp.broadcast_to(row, (chunk, LANES)).T

    for s in range(n_z):
        rows = pl.ds(s * chunk, chunk)
        keys[0, rows, :] = columns(order[s : s + 1, :])
        keys[1, rows, :] = columns(value[s : s + 1, :])
    place = lax.broadcasted_iota(jnp.int32, (chunk, LANES), 1)
    for c in range(n_z):
        total = jnp.zeros((chunk, LANES), jnp.int32)
        for s in range(n_z):
            rows = pl.ds(s * chunk, chunk)
            total = total + jnp.where(keys[0, rows, :] == place + c * LANES, keys[1, rows, :], 0)
        total = jnp.sum(total, axis=0, keepdims=True)
        inverse_v[c : c + 1, :] = total & (blocks - 1)
        packed_count[c : c + 1, :] = ((total // blocks) & (2 * LANES - 1)).astype(jnp.float32)
        kinds[c * chunk : (c + 1) * chunk, :] = columns((total // (2 * LANES * blocks)).astype(jnp.float32))
    to_scalar = pltpu.make_async_copy(inverse_v, inverse, scalar_sem)
    to_scalar.start()

    for load in loads[2:]:
        load.wait()
    for s in range(n_z):
        rows = pl.ds(s * chunk, chunk)
        ratio = jnp.exp(new[rows, :])
        weight = mask[rows, :].astype(jnp.float32) * jnp.exp(prox[rows, :])
        new[rows, :] = weight * jnp.minimum(ratio, 1.2)
        prox[rows, :] = weight * jnp.maximum(ratio, 0.8)
        returns[rows, :] = returns[rows, :] - values[rows, :]

    to_scalar.wait()
    width = 32

    def gather(i):
        z_to, first = i // (LANES // width), lax.rem(i, LANES // width) * width
        base = pl.multiple_of(i * width, width)
        for r in range(width):
            source = pl.ds(inverse[z_to, first + r], 1)
            for k, array in enumerate((returns, new, prox)):
                placed[k, pl.ds(base + r, 1), :] = array[source, :]

    pl.loop(0, 12)(gather)

    all_a = bytes_of(got_a.at[pl.ds(0, len(flat))], stat_send.at[0], stat_recv.at[0])
    all_a.wait_recv()
    merged = combine([[got_a[i, k] for k in range(3)] for i in range(2 * plane)])
    for k in range(3):
        msg_b[k] = merged[k]
        got_b[z, k] = merged[k]

    @pl.when(low)
    def _():
        pl.semaphore_wait(here_sem, half)

    for bits in (4, 5, 7, 6, 3, 2, 1):
        pltpu.make_async_remote_copy(
            src_ref=msg_b, dst_ref=got_b.at[z], send_sem=stat_send.at[1], recv_sem=stat_recv.at[1],
            device_id=along(bits), device_id_type=MESH,
        ).start()

    for o in flat:
        if o[0] == 0:
            pltpu.make_async_remote_copy(
                src_ref=packed_count, dst_ref=got_count.at[here], send_sem=count_send.at[0], recv_sem=count_recv.at[0],
                device_id=at(*o), device_id_type=MESH,
            ).start()
    got_count[here] = packed_count[...]

    pl.loop(12, blocks // width)(gather)

    all_b = bytes_of(got_b.at[pl.ds(0, n_z - 1)], stat_send.at[1], stat_recv.at[1])
    all_b.wait_recv()
    count, mean, square = combine([[got_b[i, k] for k in range(3)] for i in range(n_z)])
    scale = 1.0 / jnp.sqrt(square / jnp.maximum(count, 1.0) + 0.05)

    def spread(row, v):
        return jnp.broadcast_to(jnp.sum(jnp.where(lane == v, row, 0.0), axis=1, keepdims=True), (chunk, LANES))

    means = [spread(mean, v) for v in range(VERSIONS)]
    scales = [spread(scale, v) for v in range(VERSIONS)]

    for c in range(n_z):
        rows = pl.ds(c * chunk, chunk)
        tag_c = kinds[rows, :]
        mean_c, scale_c = means[0], scales[0]
        for v in range(1, VERSIONS):
            mean_c = jnp.where(tag_c == v, means[v], mean_c)
            scale_c = jnp.where(tag_c == v, scales[v], scale_c)
        white = (placed[0, rows, :] - mean_c) * scale_c
        factor = jnp.where(white >= 0.0, placed[1, rows, :], placed[2, rows, :])
        loss[rows, :] = -(factor * white)

    own = pl.ds(pl.multiple_of(me * per_peer, per_peer), per_peer)
    steps = [(dz, dy, dx) for dy in FAR4 for dx in FAR4 for dz in FAR8]

    for step in steps[:-1]:
        device = at(0, *step)
        there = (device[1] * plane + device[2] * n_x + device[3]) * per_peer
        pltpu.make_async_remote_copy(
            src_ref=loss.at[pl.ds(pl.multiple_of(there, per_peer), per_peer)], dst_ref=token_o.at[own],
            send_sem=token_send, recv_sem=token_recv.at[z], device_id=device, device_id_type=MESH,
        ).start()
    token_o[own, :] = loss[own, :]

    bytes_of(got_count.at[pl.ds(0, plane - 1)], count_send.at[0], count_recv.at[0]).wait_recv()
    lanes8 = lax.broadcasted_iota(jnp.int32, (n_z, LANES), 1) // per_peer
    gathered = jnp.zeros((n_z, LANES), jnp.float32)
    for p in range(plane):
        turn = lax.rem((p - here + plane) * per_peer, LANES)
        gathered = jnp.where(lanes8 == p, pltpu.roll(got_count[p], turn, 1), gathered)
    for r in range(n_z):
        count_rows[r] = gathered[r : r + 1, :]
    got_rows[z] = count_rows[z]
    for bits in range(1, n_z):
        pltpu.make_async_remote_copy(
            src_ref=count_rows.at[z ^ bits], dst_ref=got_rows.at[z], send_sem=count_send.at[1], recv_sem=count_recv.at[1],
            device_id=along(bits), device_id_type=MESH,
        ).start()

    bytes_of(token_o.at[pl.ds(0, blocks - per_peer)], token_send, token_recv.at[0]).wait_send()
    for dz in (0, 1, 7, 2, 6, 3, 5, 4):
        src = lax.rem(z + dz, n_z)
        expect = blocks // n_z - (per_peer if dz == 0 else 0)
        bytes_of(token_o.at[pl.ds(0, expect)], token_send, token_recv.at[src]).wait_recv()
        rows = pl.ds(pl.multiple_of(src * chunk, chunk), chunk)
        block_o[pl.ds(src, 1), :] = jnp.sum(token_o[rows, :].T, axis=0, keepdims=True)
    bytes_of(got_rows.at[pl.ds(0, n_z - 1)], count_send.at[1], count_recv.at[1]).wait_recv()
    for r in range(n_z):
        block_o[r : r + 1, :] = block_o[r : r + 1, :] / jnp.maximum(got_rows[r], 1.0)

    bytes_of(got_a.at[pl.ds(0, len(flat))], stat_send.at[0], stat_recv.at[0]).wait_send()
    bytes_of(got_b.at[pl.ds(0, n_z - 1)], stat_send.at[1], stat_recv.at[1]).wait_send()
    bytes_of(got_count.at[pl.ds(0, plane - 1)], count_send.at[0], count_recv.at[0]).wait_send()
    bytes_of(got_rows.at[pl.ds(0, n_z - 1)], count_send.at[1], count_recv.at[1]).wait_send()


def store(token_v, block_v, token_o, block_o, sem):
    copies = [pltpu.make_async_copy(token_v, token_o, sem.at[0]), pltpu.make_async_copy(block_v, block_o, sem.at[1])]
    for copy in copies:
        copy.start()
    for copy in copies:
        copy.wait()


def on_device(version_tags, packed_pos, valid_mask, returns, values, log_ratio_new, log_ratio_prox):
    blocks, tokens = valid_mask.shape
    n_z, n_y, n_x = (lax.axis_size(name) for name in AXES[1:])
    plane = n_y * n_x
    f32, i32 = jnp.float32, jnp.int32
    vmem, dma = pltpu.VMEM, pltpu.SemaphoreType.DMA
    small = (blocks // LANES, LANES)
    token_loss, block_loss = pl.pallas_call(
        kernel,
        out_shape=(pltpu.VMEM((blocks, tokens), f32), pltpu.VMEM(small, f32)),
        in_specs=[pl.BlockSpec(memory_space=pltpu.HBM)] * 7,
        out_specs=[pl.BlockSpec(memory_space=pltpu.VMEM)] * 2,
        scratch_shapes=[
            vmem(small, i32), vmem(small, i32), vmem((blocks, tokens), i32),
            *[vmem((blocks, tokens), f32)] * 4,
            vmem((3, *small), f32), vmem(small, i32), vmem((2, blocks, LANES), i32), vmem((blocks, LANES), f32), vmem((3, blocks, LANES), f32), vmem((blocks, LANES), f32),
            vmem(small, i32), pltpu.SMEM(small, i32),
            vmem((3, 1, LANES), f32), vmem((3, 1, LANES), f32), vmem((2 * plane, 3, 1, LANES), f32), vmem((n_z, 3, 1, LANES), f32),
            vmem(small, f32), vmem((plane, *small), f32), vmem((n_z, 1, LANES), f32), vmem((n_z, 1, LANES), f32),
            pltpu.SemaphoreType.REGULAR, dma((12,)), dma((4,)), dma, dma((2,)), dma((2,)), dma((2,)), dma((2,)), dma, dma((n_z,)),
        ],
        compiler_params=pltpu.CompilerParams(collective_id=0, has_side_effects=True, vmem_limit_bytes=32 * 2**20),
    )(*[pltpu.with_memory_space_constraint(a, pltpu.HBM) for a in (version_tags.reshape(small), packed_pos.reshape(small), valid_mask, returns, values, log_ratio_new, log_ratio_prox)])
    token_loss, block_loss = pl.pallas_call(
        store,
        out_shape=(pltpu.HBM((blocks, tokens), f32), pltpu.HBM(small, f32)),
        in_specs=[pl.BlockSpec(memory_space=pltpu.VMEM)] * 2,
        out_specs=[pl.BlockSpec(memory_space=pltpu.HBM)] * 2,
        scratch_shapes=[dma((2,))],
    )(*[pltpu.with_memory_space_constraint(a, pltpu.VMEM) for a in (token_loss, block_loss)])
    return token_loss, block_loss.reshape(blocks)


def solution(mesh):
    split = Mesh(mesh.devices.reshape(mesh.shape["grp"], 8, 4, 4), AXES)
    row, flat = P(AXES, None), P(AXES)
    return jax.shard_map(
        on_device,
        mesh=split,
        in_specs=(flat, flat, row, row, row, row, row),
        out_specs=(row, flat),
        check_vma=False,
    )
```

time: 40.1 us -> 34.4 us (0.86)
  the two profiles are of different devices: /device:TPU:1 before, /device:TPU:32 now
where the time goes in v2:
time: 34.4 us; the launch traced here: 33.9 us
  Pallas kernels  33.3 us (97%)
  between operations  0.64 us (2%)
    pallas_call x1, Pallas kernels, on_device(): pl.pallas_call(kernel, out_shape=(pltpu.VMEM((blocks, tokens), f32), pltp...  32.5 us
    pallas_call x1, Pallas kernels, on_device(): pl.pallas_call(store, out_shape=(pltpu.HBM((blocks, tokens), f32), pltpu....  0.81 us

profile of v2, /device:TPU:32, one launch (start us, length us, event | category | flops | bytes accessed | tf_op | source)
XLA Modules:
  0.0 33.9 jit_solution(13229159483971176192)
XLA Ops:
  0.6 32.5 %shard_map.86 = (f32[1024,128]{1,0:T(8,128)S(1)}, f32[8,128]{1,0:T(8,128)S(1)}) custom-call(s32[8,128]{1,0:T(8,128)} %bitcast.3, s32[8,128]{1,0:T(8,128)} %bitcast.4, s32[1024,128]{1,0:T(8,128)} %mask_h.1, f32[1024,128]{1,0:T(8,128)} %returns_h.1, f32[1024,128]{1,0:T(8,128)} %values_h.1, f32[1024,128]{1,0:T(8,128)} %new_h.1, f32[1024,128]{1,0:T(8,128)} %prox_h.1), custom_call_target="tpu_custom_call" | custom-call | tf_op jit(solution)/shard_map/pallas_call | solution.py:292
  33.1 0.8 %shard_map.87 = (f32[1024,128]{1,0:T(8,128)}, f32[8,128]{1,0:T(8,128)}) custom-call(f32[1024,128]{1,0:T(8,128)S(1)} %get-tuple-element.6.token_v, f32[8,128]{1,0:T(8,128)S(1)} %get-tuple-element.7.block_v), custom_call_target="tpu_custom_call" | custom-call | tf_op jit(solution)/shard_map/pallas_call | solution.py:308

commit v3 on v2

--- a/solution.py
+++ b/solution.py
@@ -46,7 +46,7 @@
     here = y * n_x + x
     me = z * plane + here
 
-    parts = 4
+    parts = 2
     part = blocks // parts
     stat_loads = [
         [
@@ -158,6 +158,14 @@
     to_scalar = pltpu.make_async_copy(inverse_v, inverse, scalar_sem)
     to_scalar.start()
 
+    for o in flat:
+        if o[0] == 0:
+            pltpu.make_async_remote_copy(
+                src_ref=packed_count, dst_ref=got_count.at[here], send_sem=count_send.at[0], recv_sem=count_recv.at[0],
+                device_id=at(*o), device_id_type=MESH,
+            ).start()
+    got_count[here] = packed_count[...]
+
     for load in loads[2:]:
         load.wait()
     for s in range(n_z):
@@ -198,49 +206,7 @@
             device_id=along(bits), device_id_type=MESH,
         ).start()
 
-    for o in flat:
-        if o[0] == 0:
-            pltpu.make_async_remote_copy(
-                src_ref=packed_count, dst_ref=got_count.at[here], send_sem=count_send.at[0], recv_sem=count_recv.at[0],
-                device_id=at(*o), device_id_type=MESH,
-            ).start()
-    got_count[here] = packed_count[...]
-
     pl.loop(12, blocks // width)(gather)
-
-    all_b = bytes_of(got_b.at[pl.ds(0, n_z - 1)], stat_send.at[1], stat_recv.at[1])
-    all_b.wait_recv()
-    count, mean, square = combine([[got_b[i, k] for k in range(3)] for i in range(n_z)])
-    scale = 1.0 / jnp.sqrt(square / jnp.maximum(count, 1.0) + 0.05)
-
-    def spread(row, v):
-        return jnp.broadcast_to(jnp.sum(jnp.where(lane == v, row, 0.0), axis=1, keepdims=True), (chunk, LANES))
-
-    means = [spread(mean, v) for v in range(VERSIONS)]
-    scales = [spread(scale, v) for v in range(VERSIONS)]
-
-    for c in range(n_z):
-        rows = pl.ds(c * chunk, chunk)
-        tag_c = kinds[rows, :]
-        mean_c, scale_c = means[0], scales[0]
-        for v in range(1, VERSIONS):
-            mean_c = jnp.where(tag_c == v, means[v], mean_c)
-            scale_c = jnp.where(tag_c == v, scales[v], scale_c)
-        white = (placed[0, rows, :] - mean_c) * scale_c
-        factor = jnp.where(white >= 0.0, placed[1, rows, :], placed[2, rows, :])
-        loss[rows, :] = -(factor * white)
-
-    own = pl.ds(pl.multiple_of(me * per_peer, per_peer), per_peer)
-    steps = [(dz, dy, dx) for dy in FAR4 for dx in FAR4 for dz in FAR8]
-
-    for step in steps[:-1]:
-        device = at(0, *step)
-        there = (device[1] * plane + device[2] * n_x + device[3]) * per_peer
-        pltpu.make_async_remote_copy(
-            src_ref=loss.at[pl.ds(pl.multiple_of(there, per_peer), per_peer)], dst_ref=token_o.at[own],
-            send_sem=token_send, recv_sem=token_recv.at[z], device_id=device, device_id_type=MESH,
-        ).start()
-    token_o[own, :] = loss[own, :]
 
     bytes_of(got_count.at[pl.ds(0, plane - 1)], count_send.at[0], count_recv.at[0]).wait_recv()
     lanes8 = lax.broadcasted_iota(jnp.int32, (n_z, LANES), 1) // per_peer
@@ -256,6 +222,53 @@
             src_ref=count_rows.at[z ^ bits], dst_ref=got_rows.at[z], send_sem=count_send.at[1], recv_sem=count_recv.at[1],
             device_id=along(bits), device_id_type=MESH,
         ).start()
+
+    all_b = bytes_of(got_b.at[pl.ds(0, n_z - 1)], stat_send.at[1], stat_recv.at[1])
+    all_b.wait_recv()
+    count, mean, square = combine([[got_b[i, k] for k in range(3)] for i in range(n_z)])
+    scale = 1.0 / jnp.sqrt(square / jnp.maximum(count, 1.0) + 0.05)
+
+    def spread(row, v):
+        return jnp.broadcast_to(jnp.sum(jnp.where(lane == v, row, 0.0), axis=1, keepdims=True), (strip, LANES))
+
+    strip = chunk // n_y
+    means = [spread(mean, v) for v in range(VERSIONS)]
+    scales = [spread(scale, v) for v in range(VERSIONS)]
+
+    own = pl.ds(pl.multiple_of(me * per_peer, per_peer), per_peer)
+
+    def finish(dy):
+        for c in range(n_z):
+            rows = pl.ds(pl.multiple_of(c * chunk + ((y + dy) & (n_y - 1)) * strip, strip), strip)
+            tag_c = kinds[rows, :]
+            mean_c, scale_c = means[0], scales[0]
+            for v in range(1, VERSIONS):
+                mean_c = jnp.where(tag_c == v, means[v], mean_c)
+                scale_c = jnp.where(tag_c == v, scales[v], scale_c)
+            white = (placed[0, rows, :] - mean_c) * scale_c
+            factor = jnp.where(white >= 0.0, placed[1, rows, :], placed[2, rows, :])
+            loss[rows, :] = -(factor * white)
+
+    def send(dy):
+        for dx in FAR4:
+            for dz in FAR8:
+                if (dz, dy, dx) != (0, 0, 0):
+                    device = at(0, dz, dy, dx)
+                    there = (device[1] * plane + device[2] * n_x + device[3]) * per_peer
+                    pltpu.make_async_remote_copy(
+                        src_ref=loss.at[pl.ds(pl.multiple_of(there, per_peer), per_peer)], dst_ref=token_o.at[own],
+                        send_sem=token_send, recv_sem=token_recv.at[z], device_id=device, device_id_type=MESH,
+                    ).start()
+
+    finish(FAR4[0])
+    finish(FAR4[1])
+    send(FAR4[0])
+    finish(FAR4[2])
+    send(FAR4[1])
+    finish(FAR4[3])
+    send(FAR4[2])
+    send(FAR4[3])
+    token_o[own, :] = loss[own, :]
 
     bytes_of(token_o.at[pl.ds(0, blocks - per_peer)], token_send, token_recv.at[0]).wait_send()
     for dz in (0, 1, 7, 2, 6, 3, 5, 4):
@@ -301,7 +314,7 @@
             vmem(small, i32), pltpu.SMEM(small, i32),
             vmem((3, 1, LANES), f32), vmem((3, 1, LANES), f32), vmem((2 * plane, 3, 1, LANES), f32), vmem((n_z, 3, 1, LANES), f32),
             vmem(small, f32), vmem((plane, *small), f32), vmem((n_z, 1, LANES), f32), vmem((n_z, 1, LANES), f32),
-            pltpu.SemaphoreType.REGULAR, dma((12,)), dma((4,)), dma, dma((2,)), dma((2,)), dma((2,)), dma((2,)), dma, dma((n_z,)),
+            pltpu.SemaphoreType.REGULAR, dma((6,)), dma((4,)), dma, dma((2,)), dma((2,)), dma((2,)), dma((2,)), dma, dma((n_z,)),
         ],
         compiler_params=pltpu.CompilerParams(collective_id=0, has_side_effects=True, vmem_limit_bytes=32 * 2**20),
     )(*[pltpu.with_memory_space_constraint(a, pltpu.HBM) for a in (version_tags.reshape(small), packed_pos.reshape(small), valid_mask, returns, values, log_ratio_new, log_ratio_prox)])

time: 34.4 us -> 33.7 us (0.980); the launches traced: 33.9 us -> 33.6 us
  no operation moved by 1% of the time
where the time goes in v3:
time: 33.7 us; the launch traced here: 33.6 us
  Pallas kernels  33 us (98%)
  between operations  0.64 us (2%)
    pallas_call x1, Pallas kernels, on_device(): pl.pallas_call(kernel, out_shape=(pltpu.VMEM((blocks, tokens), f32), pltp...  32.2 us
    pallas_call x1, Pallas kernels, on_device(): pl.pallas_call(store, out_shape=(pltpu.HBM((blocks, tokens), f32), pltpu....  0.81 us

profile of v3, /device:TPU:32, one launch (start us, length us, event | category | flops | bytes accessed | tf_op | source)
XLA Modules:
  0.0 33.6 jit_solution(16760712755369680246)
XLA Ops:
  0.6 32.2 %shard_map.86 = (f32[1024,128]{1,0:T(8,128)S(1)}, f32[8,128]{1,0:T(8,128)S(1)}) custom-call(s32[8,128]{1,0:T(8,128)} %bitcast.3, s32[8,128]{1,0:T(8,128)} %bitcast.4, s32[1024,128]{1,0:T(8,128)} %mask_h.1, f32[1024,128]{1,0:T(8,128)} %returns_h.1, f32[1024,128]{1,0:T(8,128)} %values_h.1, f32[1024,128]{1,0:T(8,128)} %new_h.1, f32[1024,128]{1,0:T(8,128)} %prox_h.1), custom_call_target="tpu_custom_call" | custom-call | tf_op jit(solution)/shard_map/pallas_call | solution.py:305
  32.8 0.8 %shard_map.87 = (f32[1024,128]{1,0:T(8,128)}, f32[8,128]{1,0:T(8,128)}) custom-call(f32[1024,128]{1,0:T(8,128)S(1)} %get-tuple-element.6.token_v, f32[8,128]{1,0:T(8,128)S(1)} %get-tuple-element.7.block_v), custom_call_target="tpu_custom_call" | custom-call | tf_op jit(solution)/shard_map/pallas_call | solution.py:321

commit v4 on v3

--- a/solution.py
+++ b/solution.py
@@ -270,17 +270,17 @@
     send(FAR4[3])
     token_o[own, :] = loss[own, :]
 
+    bytes_of(got_rows.at[pl.ds(0, n_z - 1)], count_send.at[1], count_recv.at[1]).wait_recv()
+    for together in ((0,), (1, 7), (2, 6), (3, 5, 4)):
+        sources = [lax.rem(z + dz, n_z) for dz in together]
+        for dz, src in zip(together, sources):
+            expect = blocks // n_z - (per_peer if dz == 0 else 0)
+            bytes_of(token_o.at[pl.ds(0, expect)], token_send, token_recv.at[src]).wait_recv()
+        arrived = [token_o[pl.ds(pl.multiple_of(src * chunk, chunk), chunk), :] for src in sources]
+        sums = [jnp.sum(rows.T, axis=0, keepdims=True) for rows in arrived]
+        for src, total in zip(sources, sums):
+            block_o[pl.ds(src, 1), :] = total / jnp.maximum(got_rows[src], 1.0)
     bytes_of(token_o.at[pl.ds(0, blocks - per_peer)], token_send, token_recv.at[0]).wait_send()
-    for dz in (0, 1, 7, 2, 6, 3, 5, 4):
-        src = lax.rem(z + dz, n_z)
-        expect = blocks // n_z - (per_peer if dz == 0 else 0)
-        bytes_of(token_o.at[pl.ds(0, expect)], token_send, token_recv.at[src]).wait_recv()
-        rows = pl.ds(pl.multiple_of(src * chunk, chunk), chunk)
-        block_o[pl.ds(src, 1), :] = jnp.sum(token_o[rows, :].T, axis=0, keepdims=True)
-    bytes_of(got_rows.at[pl.ds(0, n_z - 1)], count_send.at[1], count_recv.at[1]).wait_recv()
-    for r in range(n_z):
-        block_o[r : r + 1, :] = block_o[r : r + 1, :] / jnp.maximum(got_rows[r], 1.0)
-
     bytes_of(got_a.at[pl.ds(0, len(flat))], stat_send.at[0], stat_recv.at[0]).wait_send()
     bytes_of(got_b.at[pl.ds(0, n_z - 1)], stat_send.at[1], stat_recv.at[1]).wait_send()
     bytes_of(got_count.at[pl.ds(0, plane - 1)], count_send.at[0], count_recv.at[0]).wait_send()

time: 33.7 us -> 33.8 us (level)
  no operation moved by 1% of the time
where the time goes in v4:
time: 33.8 us; the launch traced here: 33.6 us
  Pallas kernels  33 us (98%)
  between operations  0.64 us (2%)
    pallas_call x1, Pallas kernels, on_device(): pl.pallas_call(kernel, out_shape=(pltpu.VMEM((blocks, tokens), f32), pltp...  32.2 us
    pallas_call x1, Pallas kernels, on_device(): pl.pallas_call(store, out_shape=(pltpu.HBM((blocks, tokens), f32), pltpu....  0.81 us

profile of v4, /device:TPU:32, one launch (start us, length us, event | category | flops | bytes accessed | tf_op | source)
XLA Modules:
  0.0 33.6 jit_solution(4554115814371732514)
XLA Ops:
  0.6 32.2 %shard_map.86 = (f32[1024,128]{1,0:T(8,128)S(1)}, f32[8,128]{1,0:T(8,128)S(1)}) custom-call(s32[8,128]{1,0:T(8,128)} %bitcast.3, s32[8,128]{1,0:T(8,128)} %bitcast.4, s32[1024,128]{1,0:T(8,128)} %mask_h.1, f32[1024,128]{1,0:T(8,128)} %returns_h.1, f32[1024,128]{1,0:T(8,128)} %values_h.1, f32[1024,128]{1,0:T(8,128)} %new_h.1, f32[1024,128]{1,0:T(8,128)} %prox_h.1), custom_call_target="tpu_custom_call" | custom-call | tf_op jit(solution)/shard_map/pallas_call | solution.py:305
  32.8 0.8 %shard_map.87 = (f32[1024,128]{1,0:T(8,128)}, f32[8,128]{1,0:T(8,128)}) custom-call(f32[1024,128]{1,0:T(8,128)S(1)} %get-tuple-element.6.token_v, f32[8,128]{1,0:T(8,128)S(1)} %get-tuple-element.7.block_v), custom_call_target="tpu_custom_call" | custom-call | tf_op jit(solution)/shard_map/pallas_call | solution.py:321

commit v5 on v4

--- a/solution.py
+++ b/solution.py
@@ -106,10 +106,12 @@
     tag = tags[...]
     count, mean, square = per_block[0], per_block[1], per_block[2]
     local = [jnp.zeros((1, LANES), jnp.float32)] * 3
+    stacked = [jnp.sum(jnp.where(tag == v, part, 0.0), axis=0, keepdims=True) for part in (count, count * mean) for v in range(VERSIONS)]
+    totals = jnp.sum(jnp.concatenate(stacked, axis=0), axis=1, keepdims=True)
     for v in range(VERSIONS):
         mine = tag == v
-        count_v = total_of(jnp.where(mine, count, 0.0))
-        mean_v = total_of(jnp.where(mine, count * mean, 0.0)) / jnp.maximum(count_v, 1.0)
+        count_v = totals[v : v + 1, :]
+        mean_v = totals[VERSIONS + v : VERSIONS + v + 1, :] / jnp.maximum(count_v, 1.0)
         square_v = total_of(jnp.where(mine, square + count * (mean - mean_v) * (mean - mean_v), 0.0))
         local = [jnp.where(lane == v, new_value, old) for new_value, old in zip((count_v, mean_v, square_v), local)]
     own_a = g * plane + here

time: 33.8 us -> 33.8 us (level)
  no operation moved by 1% of the time
where the time goes in v5:
time: 33.8 us; the launch traced here: 33.6 us
  Pallas kernels  33 us (98%)
  between operations  0.64 us (2%)
    pallas_call x1, Pallas kernels, on_device(): pl.pallas_call(kernel, out_shape=(pltpu.VMEM((blocks, tokens), f32), pltp...  32.2 us
    pallas_call x1, Pallas kernels, on_device(): pl.pallas_call(store, out_shape=(pltpu.HBM((blocks, tokens), f32), pltpu....  0.81 us

profile of v5, /device:TPU:32, one launch (start us, length us, event | category | flops | bytes accessed | tf_op | source)
XLA Modules:
  0.0 33.6 jit_solution(1080003577198195326)
XLA Ops:
  0.6 32.2 %shard_map.86 = (f32[1024,128]{1,0:T(8,128)S(1)}, f32[8,128]{1,0:T(8,128)S(1)}) custom-call(s32[8,128]{1,0:T(8,128)} %bitcast.3, s32[8,128]{1,0:T(8,128)} %bitcast.4, s32[1024,128]{1,0:T(8,128)} %mask_h.1, f32[1024,128]{1,0:T(8,128)} %returns_h.1, f32[1024,128]{1,0:T(8,128)} %values_h.1, f32[1024,128]{1,0:T(8,128)} %new_h.1, f32[1024,128]{1,0:T(8,128)} %prox_h.1), custom_call_target="tpu_custom_call" | custom-call | tf_op jit(solution)/shard_map/pallas_call | solution.py:307
  32.8 0.8 %shard_map.87 = (f32[1024,128]{1,0:T(8,128)}, f32[8,128]{1,0:T(8,128)}) custom-call(f32[1024,128]{1,0:T(8,128)S(1)} %get-tuple-element.6.token_v, f32[8,128]{1,0:T(8,128)S(1)} %get-tuple-element.7.block_v), custom_call_target="tpu_custom_call" | custom-call | tf_op jit(solution)/shard_map/pallas_call | solution.py:323
